TPU v7x, 32 devices: a whole 2x2x4 slice. The times are simulated.
32 devices in a mesh: study: 2 (over x), ky: 16 (over z, y, core).
Axes of the slice: x: 2, y: 2, z: 4, core: 2. Of those that a mesh axis runs over, the one named last changes fastest.
Arguments:
- kspace: bfloat16 [32, 2, 32, 256, 256], P('study', None, None, 'ky'), parts along dimension 0, may hold values from -6 to 6
- kernel: bfloat16 [2, 768, 64], replicated, may hold values from -0.21875 to 0.21875
- pattern: int32 [32], P('study'), parts along dimension 0, may hold values from 0 to 2
- offsets: int32 [4], replicated, may hold values from -2 to 2
- segment: int32 [256], replicated, may hold values from 0 to 2
- temporal_basis: float32 [5, 16], replicated, may hold values from -1.5 to 1.5
Outputs:
- basis_images: float32 [10, 2, 32, 256, 256], P('study', None, None, 'ky'), parts along dimension 0
There are 2 independent parts, one for each index of `study`. A program takes and returns all parts, laid end to end along the dimension named above; an argument that names none is the same for every part. Nothing has to cross between parts.
All inputs are finite; a program needn't handle non-finite values.
Results may differ from a plain program's by a relative error of at most 0.0003.
Values may be sent and summed in bfloat16 or wider, within the bound.
No kernel may reach another device: no remote copies, remote signals or barrier semaphores. Data moves between devices by JAX's collectives and lax.ppermute only.
A program may use at most 192 MiB of HBM per device.

v0:
```python
import jax
import jax.numpy as jnp
from jax import lax
from jax.sharding import PartitionSpec as P

frame_block = 4


def padded_2(block, sides, width):
    for axis, dim in sides:
        count = lax.axis_size(axis)
        forward = [(i, i + 1) for i in range(count - 1)]
        backward = [(target, source) for source, target in forward]
        low = lax.ppermute(
            lax.slice_in_dim(block, block.shape[dim] - width, None, axis=dim), axis, forward
        )
        high = lax.ppermute(lax.slice_in_dim(block, 0, width, axis=dim), axis, backward)
        block = jnp.concatenate([low, block, high], axis=dim)
    return block


def inverse_rows(spectra):
    row_total = spectra.shape[3]
    row_index = jnp.arange(row_total, dtype=jnp.int32)
    phase_index = row_index[:, None] * row_index[None, :] % row_total
    phase_angle = phase_index.astype(jnp.float32) * (2.0 * jnp.pi / row_total)
    cosine_table = jnp.cos(phase_angle)
    sine_table = jnp.sin(phase_angle)
    real_part = spectra[:, 0]
    imag_part = spectra[:, 1]
    high = lax.Precision.HIGHEST
    out_real = jnp.einsum("yk,mckx->mcxy", cosine_table, real_part, precision=high) - jnp.einsum(
        "yk,mckx->mcxy", sine_table, imag_part, precision=high
    )
    out_imag = jnp.einsum("yk,mckx->mcxy", sine_table, real_part, precision=high) + jnp.einsum(
        "yk,mckx->mcxy", cosine_table, imag_part, precision=high
    )
    scale = 1.0 / jnp.sqrt(jnp.float32(row_total))
    return jnp.stack([out_real, out_imag], axis=1) * scale


def on_device(kspace, kernel, pattern, offsets, segment, temporal_basis):
    frame_total, _, coil_count, row_count, kx_count = kspace.shape
    group_count = kernel.shape[0]
    group_frames = frame_total // group_count
    row_start = lax.axis_index("ky") * row_count
    local_segment = lax.dynamic_slice_in_dim(segment, row_start, row_count)
    acquired = (local_segment[None, :] == pattern[:, None])[:, None, None, :, None]
    zero_fill = jnp.where(acquired, kspace, jnp.zeros_like(kspace))
    padded = padded_2(zero_fill, (("ky", 3),), 1)
    blocks = frame_total // frame_block
    padded_blocks = padded.reshape(blocks, frame_block, 2, coil_count, row_count + 2, kx_count)
    block_group = jnp.arange(blocks, dtype=jnp.int32) * frame_block // group_frames

    def estimate_block(block_item):
        block_data, group_index = block_item
        ky_layers = []
        for ky_tap in range(3):
            ky_slice = block_data[:, :, :, ky_tap : ky_tap + row_count, :]
            ky_layers.append(
                jnp.stack(
                    [
                        jnp.roll(ky_slice, -offsets[kx_tap], axis=4)
                        for kx_tap in range(offsets.shape[0])
                    ],
                    axis=2,
                )
            )
        sources = jnp.stack(ky_layers, axis=2).reshape(frame_block, -1, row_count * kx_count)
        weights = lax.dynamic_index_in_dim(kernel, group_index, 0, keepdims=False)
        return jnp.einsum("io,fir->for", weights, sources, preferred_element_type=jnp.float32)

    estimate = lax.map(estimate_block, (padded_blocks, block_group))
    estimate = estimate.reshape(frame_total, 2, coil_count, row_count, kx_count)
    filled = jnp.where(acquired, kspace.astype(jnp.float32), estimate)
    high = lax.Precision.HIGHEST
    coefficients = jnp.einsum("bf,fpcrx->bpcrx", temporal_basis, filled, precision=high)
    swapped = lax.all_to_all(coefficients, "ky", split_axis=4, concat_axis=3, tiled=True)
    return inverse_rows(swapped)


def solution(mesh):
    return jax.shard_map(
        on_device,
        mesh=mesh,
        in_specs=(P("study", None, None, "ky", None), P(), P("study"), P(), P(), P()),
        out_specs=P("study", None, None, "ky", None),
        check_vma=False,
    )
```

profile of v0, /device:TPU:1, one launch (start us, length us, event | category | flops | bytes accessed | tf_op | source)
XLA Modules:
  0.0 754.4 jit_solution(11994539295915836448)
XLA Ops:
  31.8 13.5 %pad_maximum_fusion.1 = bf16[16,2,32,18,256]{4,3,2,1,0:T(8,128)(2,1)} fusion(bf16[16,2,32,1,256]{4,3,2,1,0:T(2,128)(2,1)S(1)} %copy.40, bf16[16,2,32,16,256]{4,3,2,1,0:T(8,128)(2,1)} %broadcast_select_fusion, bf16[16,2,32,1,256]{4,3,2,1,0:T(2,128)(2,1)S(1)} %copy.39), kind=kLoop, calls=%fused_computation.61 | loop fusion | flops 28311552 | bytes 18874368 | tf_op jit(solution)/shard_map/concatenate | solution.py:18
  45.4 419.9 %while.12 = (s32[]{:T(128)}, f32[4,4,64,4096]{3,2,1,0:T(8,128)}, bf16[4,4,2,32,18,256]{5,4,3,2,1,0:T(8,128)(2,1)}, s32[]{:T(128)}, s32[]{:T(128)}, /*index=5*/s3...) while((s32[]{:T(128)}, f32[4,4,64,4096]{3,2,1,0:T(8,128)}, ...), condition=%wide.region_1.3_spmd, body=%wide.region_0.2_spmd.sunk | while | flops 1723858944 | bytes 229213552 | solution.py:73
  57.6 9.1 %fusion.95 = (bf16[4,2,1,32,16,256]{5,4,3,2,1,0:T(8,128)(2,1)}, bf16[4,2,1,32,16,256]{5,4,3,2,1,0:T(8,128)(2,1)}, bf16[4,2,1,32,16,256]{5,4,3,2,1,0:T(8,128)(2,1)}, bf16[4,2,1,32,16,256]{5,4,3,2,1,0:T(8,128)(2,1)}) fusion(s32[]{:T(128)S(6)} %select_n.129, bf16[4,2,32,16,256]{4,3,2,1,0:T(8,128)(2,1)S(1)} %get-tuple-element.228, s32[]{:T(128)S(6)} %select_n.131, ...), kind=kLoop, calls=%fused_computation.42.clone.1 | loop fusion | flops 16777216 | bytes 10485776 | tf_op jit(solution)/shard_map/while/body/eval_jaxpr/stack | solution.py:61
  72.6 11.5 %fusion.93 = (bf16[4,2,1,32,16,256]{5,4,3,2,1,0:T(8,128)(2,1)S(1)}, bf16[4,2,1,32,16,256]{5,4,3,2,1,0:T(8,128)(2,1)S(1)}, bf16[4,2,1,32,16,256]{5,4,3,2,1,0:T(8,128)(2,1)S(1)}, bf16[4,2,1,32,16,256]{5,4,3,2,1,0:T(8,128)(2,1)S(1)}) fusion(s32[]{:T(128)S(6)} %select_n.129, bf16[4,2,32,16,256]{4,3,2,1,0:T(8,128)(2,1)} %get-tuple-element.218, ...), kind=kLoop, calls=%fused_computation.34.clone.1 | loop fusion | flops 16777216 | bytes 10485776 | tf_op jit(solution)/shard_map/while/body/eval_jaxpr/stack | solution.py:61
  85.2 10.2 %pad_maximum_fusion.3 = bf16[4,2,3,4,32,16,256]{6,5,4,3,2,1,0:T(8,128)(2,1)} fusion(bf16[4,2,1,4,32,16,256]{6,5,4,3,2,1,0:T(8,128)(2,1)S(1)} %maximum_bitcast_fusion.5, bf16[4,2,1,4,32,16,256]{6,5,4,3,2,1,0:T(8,128)(2,1)S(1)} %get-tuple-element.233, bf16[4,2,1,4,32,16,256]{6,5,4,3,2,1,0:T(8,128)(2,1)S(1)} %get-tuple-element.234), kind=kLoop, calls=%fused_computation.clone.1 | loop fusion | flops 25165824 | bytes 50331648 | tf_op jit(solution)/shard_map/while/body/eval_jaxpr/stack | solution.py:69
  95.4 37.8 %reshape.50 = bf16[4,768,4096]{2,1,0:T(8,128)(2,1)} reshape(bf16[4,2,3,4,32,16,256]{6,5,4,3,2,1,0:T(8,128)(2,1)} %pad_maximum_fusion.3) | data formatting | bytes 50331648 | tf_op jit(solution)/shard_map/while/body/eval_jaxpr/reshape | solution.py:69
  135.8 14.8 %fusion.96 = f32[4,4,64,4096]{3,2,1,0:T(8,128)} fusion(f32[4,4,64,4096]{3,2,1,0:T(8,128)} %get-tuple-element.251, s32[]{:T(128)} %get-tuple-element.250, bf16[4,768,4096]{2,1,0:T(8,128)(2,1)} %reshape.50, bf16[2,768,64]{1,2,0:T(8,128)(2,1)S(1)} %get-tuple-element.273, s32[]{:T(128)S(6)} %select_n.136), kind=kOutput, calls=%fused_computation.29.clone.1 | convolution fusion | flops 1610612736 | bytes 29458948 | tf_op jit(solution)/shard_map/while/body/eval_jaxpr/io,fir->for/dot_general | solution.py:71
  162.5 9.1 %fusion.95 = (bf16[4,2,1,32,16,256]{5,4,3,2,1,0:T(8,128)(2,1)}, bf16[4,2,1,32,16,256]{5,4,3,2,1,0:T(8,128)(2,1)}, bf16[4,2,1,32,16,256]{5,4,3,2,1,0:T(8,128)(2,1)}, bf16[4,2,1,32,16,256]{5,4,3,2,1,0:T(8,128)(2,1)}) fusion(s32[]{:T(128)S(6)} %select_n.129, bf16[4,2,32,16,256]{4,3,2,1,0:T(8,128)(2,1)S(1)} %get-tuple-element.228, s32[]{:T(128)S(6)} %select_n.131, ...), kind=kLoop, calls=%fused_computation.42.clone.1 | loop fusion | flops 16777216 | bytes 10485776 | tf_op jit(solution)/shard_map/while/body/eval_jaxpr/stack | solution.py:61
  177.5 11.5 %fusion.93 = (bf16[4,2,1,32,16,256]{5,4,3,2,1,0:T(8,128)(2,1)S(1)}, bf16[4,2,1,32,16,256]{5,4,3,2,1,0:T(8,128)(2,1)S(1)}, bf16[4,2,1,32,16,256]{5,4,3,2,1,0:T(8,128)(2,1)S(1)}, bf16[4,2,1,32,16,256]{5,4,3,2,1,0:T(8,128)(2,1)S(1)}) fusion(s32[]{:T(128)S(6)} %select_n.129, bf16[4,2,32,16,256]{4,3,2,1,0:T(8,128)(2,1)} %get-tuple-element.218, ...), kind=kLoop, calls=%fused_computation.34.clone.1 | loop fusion | flops 16777216 | bytes 10485776 | tf_op jit(solution)/shard_map/while/body/eval_jaxpr/stack | solution.py:61
  190.1 10.2 %pad_maximum_fusion.3 = bf16[4,2,3,4,32,16,256]{6,5,4,3,2,1,0:T(8,128)(2,1)} fusion(bf16[4,2,1,4,32,16,256]{6,5,4,3,2,1,0:T(8,128)(2,1)S(1)} %maximum_bitcast_fusion.5, bf16[4,2,1,4,32,16,256]{6,5,4,3,2,1,0:T(8,128)(2,1)S(1)} %get-tuple-element.233, bf16[4,2,1,4,32,16,256]{6,5,4,3,2,1,0:T(8,128)(2,1)S(1)} %get-tuple-element.234), kind=kLoop, calls=%fused_computation.clone.1 | loop fusion | flops 25165824 | bytes 50331648 | tf_op jit(solution)/shard_map/while/body/eval_jaxpr/stack | solution.py:69
  200.3 37.8 %reshape.50 = bf16[4,768,4096]{2,1,0:T(8,128)(2,1)} reshape(bf16[4,2,3,4,32,16,256]{6,5,4,3,2,1,0:T(8,128)(2,1)} %pad_maximum_fusion.3) | data formatting | bytes 50331648 | tf_op jit(solution)/shard_map/while/body/eval_jaxpr/reshape | solution.py:69
  240.7 14.7 %fusion.96 = f32[4,4,64,4096]{3,2,1,0:T(8,128)} fusion(f32[4,4,64,4096]{3,2,1,0:T(8,128)} %get-tuple-element.251, s32[]{:T(128)} %get-tuple-element.250, bf16[4,768,4096]{2,1,0:T(8,128)(2,1)} %reshape.50, bf16[2,768,64]{1,2,0:T(8,128)(2,1)S(1)} %get-tuple-element.273, s32[]{:T(128)S(6)} %select_n.136), kind=kOutput, calls=%fused_computation.29.clone.1 | convolution fusion | flops 1610612736 | bytes 29458948 | tf_op jit(solution)/shard_map/while/body/eval_jaxpr/io,fir->for/dot_general | solution.py:71
  267.3 9.1 %fusion.95 = (bf16[4,2,1,32,16,256]{5,4,3,2,1,0:T(8,128)(2,1)}, bf16[4,2,1,32,16,256]{5,4,3,2,1,0:T(8,128)(2,1)}, bf16[4,2,1,32,16,256]{5,4,3,2,1,0:T(8,128)(2,1)}, bf16[4,2,1,32,16,256]{5,4,3,2,1,0:T(8,128)(2,1)}) fusion(s32[]{:T(128)S(6)} %select_n.129, bf16[4,2,32,16,256]{4,3,2,1,0:T(8,128)(2,1)S(1)} %get-tuple-element.228, s32[]{:T(128)S(6)} %select_n.131, ...), kind=kLoop, calls=%fused_computation.42.clone.1 | loop fusion | flops 16777216 | bytes 10485776 | tf_op jit(solution)/shard_map/while/body/eval_jaxpr/stack | solution.py:61
  282.3 11.5 %fusion.93 = (bf16[4,2,1,32,16,256]{5,4,3,2,1,0:T(8,128)(2,1)S(1)}, bf16[4,2,1,32,16,256]{5,4,3,2,1,0:T(8,128)(2,1)S(1)}, bf16[4,2,1,32,16,256]{5,4,3,2,1,0:T(8,128)(2,1)S(1)}, bf16[4,2,1,32,16,256]{5,4,3,2,1,0:T(8,128)(2,1)S(1)}) fusion(s32[]{:T(128)S(6)} %select_n.129, bf16[4,2,32,16,256]{4,3,2,1,0:T(8,128)(2,1)} %get-tuple-element.218, ...), kind=kLoop, calls=%fused_computation.34.clone.1 | loop fusion | flops 16777216 | bytes 10485776 | tf_op jit(solution)/shard_map/while/body/eval_jaxpr/stack | solution.py:61
  294.9 10.2 %pad_maximum_fusion.3 = bf16[4,2,3,4,32,16,256]{6,5,4,3,2,1,0:T(8,128)(2,1)} fusion(bf16[4,2,1,4,32,16,256]{6,5,4,3,2,1,0:T(8,128)(2,1)S(1)} %maximum_bitcast_fusion.5, bf16[4,2,1,4,32,16,256]{6,5,4,3,2,1,0:T(8,128)(2,1)S(1)} %get-tuple-element.233, bf16[4,2,1,4,32,16,256]{6,5,4,3,2,1,0:T(8,128)(2,1)S(1)} %get-tuple-element.234), kind=kLoop, calls=%fused_computation.clone.1 | loop fusion | flops 25165824 | bytes 50331648 | tf_op jit(solution)/shard_map/while/body/eval_jaxpr/stack | solution.py:69
  305.1 37.8 %reshape.50 = bf16[4,768,4096]{2,1,0:T(8,128)(2,1)} reshape(bf16[4,2,3,4,32,16,256]{6,5,4,3,2,1,0:T(8,128)(2,1)} %pad_maximum_fusion.3) | data formatting | bytes 50331648 | tf_op jit(solution)/shard_map/while/body/eval_jaxpr/reshape | solution.py:69
  345.5 14.7 %fusion.96 = f32[4,4,64,4096]{3,2,1,0:T(8,128)} fusion(f32[4,4,64,4096]{3,2,1,0:T(8,128)} %get-tuple-element.251, s32[]{:T(128)} %get-tuple-element.250, bf16[4,768,4096]{2,1,0:T(8,128)(2,1)} %reshape.50, bf16[2,768,64]{1,2,0:T(8,128)(2,1)S(1)} %get-tuple-element.273, s32[]{:T(128)S(6)} %select_n.136), kind=kOutput, calls=%fused_computation.29.clone.1 | convolution fusion | flops 1610612736 | bytes 29458948 | tf_op jit(solution)/shard_map/while/body/eval_jaxpr/io,fir->for/dot_general | solution.py:71
  372.1 9.1 %fusion.95 = (bf16[4,2,1,32,16,256]{5,4,3,2,1,0:T(8,128)(2,1)}, bf16[4,2,1,32,16,256]{5,4,3,2,1,0:T(8,128)(2,1)}, bf16[4,2,1,32,16,256]{5,4,3,2,1,0:T(8,128)(2,1)}, bf16[4,2,1,32,16,256]{5,4,3,2,1,0:T(8,128)(2,1)}) fusion(s32[]{:T(128)S(6)} %select_n.129, bf16[4,2,32,16,256]{4,3,2,1,0:T(8,128)(2,1)S(1)} %get-tuple-element.228, s32[]{:T(128)S(6)} %select_n.131, ...), kind=kLoop, calls=%fused_computation.42.clone.1 | loop fusion | flops 16777216 | bytes 10485776 | tf_op jit(solution)/shard_map/while/body/eval_jaxpr/stack | solution.py:61
  387.1 11.5 %fusion.93 = (bf16[4,2,1,32,16,256]{5,4,3,2,1,0:T(8,128)(2,1)S(1)}, bf16[4,2,1,32,16,256]{5,4,3,2,1,0:T(8,128)(2,1)S(1)}, bf16[4,2,1,32,16,256]{5,4,3,2,1,0:T(8,128)(2,1)S(1)}, bf16[4,2,1,32,16,256]{5,4,3,2,1,0:T(8,128)(2,1)S(1)}) fusion(s32[]{:T(128)S(6)} %select_n.129, bf16[4,2,32,16,256]{4,3,2,1,0:T(8,128)(2,1)} %get-tuple-element.218, ...), kind=kLoop, calls=%fused_computation.34.clone.1 | loop fusion | flops 16777216 | bytes 10485776 | tf_op jit(solution)/shard_map/while/body/eval_jaxpr/stack | solution.py:61
  399.7 10.2 %pad_maximum_fusion.3 = bf16[4,2,3,4,32,16,256]{6,5,4,3,2,1,0:T(8,128)(2,1)} fusion(bf16[4,2,1,4,32,16,256]{6,5,4,3,2,1,0:T(8,128)(2,1)S(1)} %maximum_bitcast_fusion.5, bf16[4,2,1,4,32,16,256]{6,5,4,3,2,1,0:T(8,128)(2,1)S(1)} %get-tuple-element.233, bf16[4,2,1,4,32,16,256]{6,5,4,3,2,1,0:T(8,128)(2,1)S(1)} %get-tuple-element.234), kind=kLoop, calls=%fused_computation.clone.1 | loop fusion | flops 25165824 | bytes 50331648 | tf_op jit(solution)/shard_map/while/body/eval_jaxpr/stack | solution.py:69
  409.9 37.8 %reshape.50 = bf16[4,768,4096]{2,1,0:T(8,128)(2,1)} reshape(bf16[4,2,3,4,32,16,256]{6,5,4,3,2,1,0:T(8,128)(2,1)} %pad_maximum_fusion.3) | data formatting | bytes 50331648 | tf_op jit(solution)/shard_map/while/body/eval_jaxpr/reshape | solution.py:69
  450.2 14.7 %fusion.96 = f32[4,4,64,4096]{3,2,1,0:T(8,128)} fusion(f32[4,4,64,4096]{3,2,1,0:T(8,128)} %get-tuple-element.251, s32[]{:T(128)} %get-tuple-element.250, bf16[4,768,4096]{2,1,0:T(8,128)(2,1)} %reshape.50, bf16[2,768,64]{1,2,0:T(8,128)(2,1)S(1)} %get-tuple-element.273, s32[]{:T(128)S(6)} %select_n.136), kind=kOutput, calls=%fused_computation.29.clone.1 | convolution fusion | flops 1610612736 | bytes 29458948 | tf_op jit(solution)/shard_map/while/body/eval_jaxpr/io,fir->for/dot_general | solution.py:71
  465.3 11.0 %copy.54 = f32[128,8,16,256]{3,2,1,0:T(8,128)S(1)} copy(f32[128,8,16,256]{3,1,2,0:T(8,128)} %bitcast.126) | data formatting | bytes 33554432
  482.5 17.8 %fusion.30 = f32[5,2,32,16,256]{4,0,3,2,1:T(8,128)} fusion(f32[16,2,32,16,256]{4,3,2,1,0:T(8,128)S(1)} %convert_select_fusion, f32[5,16]{1,0:T(8,128)S(1)} %copy-done), kind=kOutput, calls=%fused_computation.64 | convolution fusion | flops 251658240 | bytes 22020416 | tf_op jit(solution)/shard_map/bf,fpcrx->bpcrx/dot_general | solution.py:77
  500.3 14.0 %copy.42 = f32[5,2,32,16,256]{2,3,1,0,4:T(8,128)} copy(f32[5,2,32,16,256]{4,0,3,2,1:T(8,128)} %fusion.30) | data formatting | bytes 10485760 | tf_op jit(solution)/shard_map/bf,fpcrx->bpcrx/dot_general | solution.py:77
  514.2 18.0 %reshape.47 = f32[16,1,81920]{2,1,0:T(1,128)} reshape(f32[256,5,2,16,32]{4,3,2,1,0:T(8,128)} %bitcast.122) | data formatting | bytes 10485760
  532.2 121.4 %all_to_all.18 = f32[16,1,81920]{2,1,0:T(1,128)} all-to-all(f32[16,1,81920]{2,1,0:T(1,128)} %reshape.47), channel_id=1, replica_groups=mesh['study'=2,'ky'=16] {'ky'}, dimensions={0} | all-to-all | bytes 10485760 | tf_op jit(solution)/shard_map/all_to_all | solution.py:78
  654.2 16.9 %reduce = f32[16,81920]{1,0:T(8,128)} reduce(f32[16,1,81920]{2,1,0:T(1,128)} %all_to_all.18, f32[]{:T(128)} %broadcast.61), dimensions={1}, to_apply=%all_to_all.13.reduce_sub_computation | reduce | bytes 10485764 | tf_op jit(solution)/shard_map/all_to_all | solution.py:78
  671.1 18.1 %reshape.48 = f32[256,5,2,16,32]{4,3,2,1,0:T(8,128)} reshape(f32[16,81920]{1,0:T(8,128)} %reduce) | data formatting | bytes 10485760
  689.2 18.5 %copy.44 = f32[5,2,32,16,16,16]{2,5,4,3,1,0:T(8,128)S(1)} copy(f32[5,2,32,16,16,16]{2,4,1,0,5,3:T(8,128)} %bitcast.123) | data formatting | bytes 10485760 | tf_op jit(solution)/shard_map/all_to_all | solution.py:78
  715.3 8.6 %copy.53 = f32[5,1,32,256,16]{3,4,2,0,1:T(8,128)S(1)} copy(f32[5,1,32,256,16]{2,4,3,1,0:T(8,128)} %get-tuple-element.139) | data formatting | bytes 5242880
  733.4 8.7 %copy.52 = f32[5,1,32,256,16]{3,4,2,0,1:T(8,128)S(1)} copy(f32[5,1,32,256,16]{2,4,3,1,0:T(8,128)} %get-tuple-element.138) | data formatting | bytes 5242880
  (60 shorter events, 143.0 us)
Async XLA Ops:
  0.0 482.5 %copy-start = (f32[5,16]{1,0:T(8,128)S(1)}, f32[5,16]{1,0:T(8,128)}, u32[]{:S(2)}) copy-start(f32[5,16]{1,0:T(8,128)} %param.15) | copy-start | bytes 964
  1.5 7.2 copy-start.3
  8.7 11.3 %copy-start.5 = (s32[4]{0:T(128)S(1)}, s32[4]{0:T(128)}, u32[]{:S(2)}) copy-start(s32[4]{0:T(128)} %param.13) | copy-start | bytes 52
  13.5 16.3 %collective-permute-start = (bf16[16,2,32,1,256]{4,2,3,1,0:T(8,128)(2,1)S(1)}, bf16[16,2,32,1,256]{4,2,3,1,0:T(8,128)(2,1)S(1)}, u32[]{:S(2)}, u32[]{:S(2)}) collective-permute-start(bf16[16,2,32,1,256]{4,2,3,1,0:T(8,128)(2,1)S(1)} %copy.37), channel_id=1, source_target_pairs={{0,1},{1,2},{2,3},{3,4},{4,5},{5,6},{6,7},{7,8},{8,9},{9,10},{10,1... | collective-permute-start | bytes 1572872 | tf_op jit(solution)/shard_map/ppermute | solution.py:14
  18.1 12.6 %collective-permute-start.1 = (bf16[16,2,32,1,256]{4,2,3,1,0:T(8,128)(2,1)S(1)}, bf16[16,2,32,1,256]{4,2,3,1,0:T(8,128)(2,1)S(1)}, u32[]{:S(2)}, u32[]{:S(2)}) collective-permute-start(bf16[16,2,32,1,256]{4,2,3,1,0:T(8,128)(2,1)S(1)} %copy.38), channel_id=1, source_target_pairs={{1,0},{2,1},{3,2},{4,3},{5,4},{6,5},{7,6},{8,7},{9,8},{10,9},{11,1... | collective-permute-start | bytes 1572872 | tf_op jit(solution)/shard_map/ppermute | solution.py:17
  31.8 13.6 %copy-start.2 = (bf16[2,768,64]{1,2,0:T(8,128)(2,1)S(1)}, bf16[2,768,64]{1,2,0:T(8,128)(2,1)}, u32[]{:S(2)}) copy-start(bf16[2,768,64]{1,2,0:T(8,128)(2,1)} %param.11) | copy-start | bytes 589828
  465.3 11.0 %copy-start.4 = (pred[16,16]{1,0:T(8,128)(4,1)S(1)}, pred[16,16]{1,0:T(8,128)(4,1)}, u32[]{:S(2)}) copy-start(pred[16,16]{1,0:T(8,128)(4,1)} %copy-done.3) | copy-start | bytes 772
  742.0 5.1 copy-start.1
where the time goes:
time: 765 us; the launch traced here: 754 us
  local copies, waits for them, and re-layouts  289 us (38%)
  other arithmetic  225 us (29%)
  blocking collectives  121 us (16%)
  matrix products  94.5 us (12%)
  loops' own time  8.59 us (1%)
    reshape x4, local copies, waits for them, and re-layouts, estimate_block(): jnp.stack(ky_layers, axis=2).reshape(frame_block, -1, row_count * kx_count)  151 us
    all_to_all x1, blocking collectives, on_device(): lax.all_to_all(coefficients, 'ky', split_axis=4, concat_axis=3, tiled=True)  121 us
    another operation x12, other arithmetic, estimate_block(): jnp.stack([jnp.roll(ky_slice, -offsets[kx_tap], axis=4) for kx_tap in ran...  111 us
    another operation x12, other arithmetic, estimate_block(): jnp.stack(ky_layers, axis=2).reshape(frame_block, -1, row_count * kx_count)  68.6 us
    unnamed x17, local copies, waits for them, and re-layouts  64.4 us
    dot_general x4, matrix products, estimate_block(): jnp.einsum('io,fir->for', weights, sources, preferred_element_type=jnp.fl...  58.8 us
    all_to_all x2, local copies, waits for them, and re-layouts, on_device(): lax.all_to_all(coefficients, 'ky', split_axis=4, concat_axis=3, tiled=True)  19 us
    dot_general x1, matrix products, on_device(): jnp.einsum('bf,fpcrx->bpcrx', temporal_basis, filled, precision=high)  17.8 us
  transfers between devices with their start and end apart: 2, of which 1 were waited for; matrix products, arithmetic and copies ran while one was open for 0% of the time, Pallas kernels for 0%

commit v1 on v0

--- a/solution.py
+++ b/solution.py
@@ -4,6 +4,21 @@
 from jax.sharding import PartitionSpec as P
 
 frame_block = 4
+
+
+def _show_spot(w_in, dim_no, frame_in):
+    lower, left_arr = (w_in.shape[:dim_no], w_in.shape[dim_no + 1 :])
+    return jnp.moveaxis(w_in.reshape(*lower, frame_in, -1, *left_arr), dim_no, 0)
+
+
+def order_trails(matrix, pos_dim):
+    matrix = jnp.moveaxis(matrix, 0, pos_dim)
+    current_block = matrix.shape
+    return matrix.reshape(
+        *current_block[:pos_dim],
+        current_block[pos_dim] * current_block[pos_dim + 1],
+        *current_block[pos_dim + 2 :]
+    )
 
 
 def padded_2(block, sides, width):
@@ -75,7 +90,18 @@
     filled = jnp.where(acquired, kspace.astype(jnp.float32), estimate)
     high = lax.Precision.HIGHEST
     coefficients = jnp.einsum("bf,fpcrx->bpcrx", temporal_basis, filled, precision=high)
-    swapped = lax.all_to_all(coefficients, "ky", split_axis=4, concat_axis=3, tiled=True)
+    finding = lax.axis_size("ky")
+    w1, s_next = (finding, lax.axis_index("ky"))
+    carry_in = _show_spot(coefficients, 4, w1)
+    u = 1
+    d_next = carry_in
+    while u < w1:
+        item_now, r2 = ((s_next + u) % w1, (s_next - u) % w1)
+        placed = lax.dynamic_index_in_dim(carry_in, item_now, 0)
+        reply = lax.ppermute(placed, "ky", perm=tuple(((d, (d + u) % w1) for d in range(w1))))
+        d_next = lax.dynamic_update_slice_in_dim(d_next, reply, r2, axis=0)
+        u = u + 1
+    swapped = order_trails(d_next, 3)
     return inverse_rows(swapped)
 
 

time: 765 us -> 1090 us (1.42)
  the two profiles are of different devices: /device:TPU:1 before, /device:TPU:9 now
where the time goes in v1:
time: 1090 us; the launch traced here: 1080 us
  starting transfers between devices  354 us (32%)
  local copies, waits for them, and re-layouts  284 us (26%)
  other arithmetic  208 us (19%)
  waiting for transfers between devices  128 us (12%)
  matrix products  94.6 us (9%)
    ppermute x15, starting transfers between devices, on_device(): lax.ppermute(placed, 'ky', perm=tuple(((d, (d + u) % w1) for d in range(w...  348 us
    reshape x4, local copies, waits for them, and re-layouts, estimate_block(): jnp.stack(ky_layers, axis=2).reshape(frame_block, -1, row_count * kx_count)  151 us
    ppermute x15, waiting for transfers between devices, on_device(): lax.ppermute(placed, 'ky', perm=tuple(((d, (d + u) % w1) for d in range(w...  121 us
    another operation x12, other arithmetic, estimate_block(): jnp.stack([jnp.roll(ky_slice, -offsets[kx_tap], axis=4) for kx_tap in ran...  111 us
    another operation x12, other arithmetic, estimate_block(): jnp.stack(ky_layers, axis=2).reshape(frame_block, -1, row_count * kx_count)  69.1 us
    dot_general x4, matrix products, estimate_block(): jnp.einsum('io,fir->for', weights, sources, preferred_element_type=jnp.fl...  58.9 us
    unnamed x27, local copies, waits for them, and re-layouts  28.1 us
    dynamic_update_slice x15, local copies, waits for them, and re-layouts, on_device(): d_next = lax.dynamic_update_slice_in_dim(d_next, reply, r2, axis=0)  22.3 us
  transfers between devices with their start and end apart: 17, of which 6 were waited for; matrix products, arithmetic and copies ran while one was open for 2% of the time, Pallas kernels for 0%

profile of v1, /device:TPU:9, one launch (start us, length us, event | category | flops | bytes accessed | tf_op | source)
XLA Modules:
  0.0 1080.1 jit_solution(7008556805317428895)
XLA Ops:
  31.8 13.5 %pad_maximum_fusion.1 = bf16[16,2,32,18,256]{4,3,2,1,0:T(8,128)(2,1)} fusion(bf16[16,2,32,1,256]{4,3,2,1,0:T(2,128)(2,1)S(1)} %copy.28, bf16[16,2,32,16,256]{4,3,2,1,0:T(8,128)(2,1)} %broadcast_select_fusion, bf16[16,2,32,1,256]{4,3,2,1,0:T(2,128)(2,1)S(1)} %copy.27), kind=kLoop, calls=%fused_computation.61 | loop fusion | flops 28311552 | bytes 18874368 | tf_op jit(solution)/shard_map/concatenate | solution.py:33
  45.3 425.0 %while.12 = (s32[]{:T(128)}, f32[4,4,64,4096]{3,2,1,0:T(8,128)}, bf16[4,4,2,32,18,256]{5,4,3,2,1,0:T(8,128)(2,1)}, s32[]{:T(128)}, s32[]{:T(128)}, /*index=5*/s3...) while((s32[]{:T(128)}, f32[4,4,64,4096]{3,2,1,0:T(8,128)}, ...), condition=%wide.region_1.3_spmd, body=%wide.region_0.2_spmd.sunk | while | flops 1723858944 | bytes 237601680 | solution.py:88
  51.1 11.5 %fusion.93 = (bf16[4,2,1,32,16,256]{5,4,3,2,1,0:T(8,128)(2,1)S(1)}, bf16[4,2,1,32,16,256]{5,4,3,2,1,0:T(8,128)(2,1)S(1)}, bf16[4,2,1,32,16,256]{5,4,3,2,1,0:T(8,128)(2,1)S(1)}, bf16[4,2,1,32,16,256]{5,4,3,2,1,0:T(8,128)(2,1)S(1)}) fusion(s32[]{:T(128)S(6)} %select_n.402, bf16[4,2,32,16,256]{4,3,2,1,0:T(8,128)(2,1)} %get-tuple-element.233, ...), kind=kLoop, calls=%fused_computation.34.clone.1 | loop fusion | flops 16777216 | bytes 10485776 | tf_op jit(solution)/shard_map/while/body/eval_jaxpr/stack | solution.py:76
  86.2 10.3 pad_maximum_fusion.3
  96.6 37.8 %reshape.71 = bf16[4,768,4096]{2,1,0:T(8,128)(2,1)} reshape(bf16[4,2,3,4,32,16,256]{6,5,4,3,2,1,0:T(8,128)(2,1)} %pad_maximum_fusion.3) | data formatting | bytes 50331648 | tf_op jit(solution)/shard_map/while/body/eval_jaxpr/reshape | solution.py:84
  136.9 14.8 %fusion.96 = f32[4,4,64,4096]{3,2,1,0:T(8,128)} fusion(f32[4,4,64,4096]{3,2,1,0:T(8,128)} %get-tuple-element.266, s32[]{:T(128)S(6)} %copy.48, bf16[4,768,4096]{2,1,0:T(8,128)(2,1)} %reshape.71, bf16[2,768,64]{1,2,0:T(8,128)(2,1)S(1)} %get-tuple-element.288, s32[]{:T(128)S(6)} %select_n.409), kind=kOutput, calls=%fused_computation.29.clone.1 | convolution fusion | flops 1610612736 | bytes 29458440 | tf_op jit(solution)/shard_map/while/body/eval_jaxpr/io,fir->for/dot_general | solution.py:86
  157.2 11.5 %fusion.93 = (bf16[4,2,1,32,16,256]{5,4,3,2,1,0:T(8,128)(2,1)S(1)}, bf16[4,2,1,32,16,256]{5,4,3,2,1,0:T(8,128)(2,1)S(1)}, bf16[4,2,1,32,16,256]{5,4,3,2,1,0:T(8,128)(2,1)S(1)}, bf16[4,2,1,32,16,256]{5,4,3,2,1,0:T(8,128)(2,1)S(1)}) fusion(s32[]{:T(128)S(6)} %select_n.402, bf16[4,2,32,16,256]{4,3,2,1,0:T(8,128)(2,1)} %get-tuple-element.233, ...), kind=kLoop, calls=%fused_computation.34.clone.1 | loop fusion | flops 16777216 | bytes 10485776 | tf_op jit(solution)/shard_map/while/body/eval_jaxpr/stack | solution.py:76
  192.4 10.3 pad_maximum_fusion.3
  202.7 37.8 %reshape.71 = bf16[4,768,4096]{2,1,0:T(8,128)(2,1)} reshape(bf16[4,2,3,4,32,16,256]{6,5,4,3,2,1,0:T(8,128)(2,1)} %pad_maximum_fusion.3) | data formatting | bytes 50331648 | tf_op jit(solution)/shard_map/while/body/eval_jaxpr/reshape | solution.py:84
  243.0 14.7 %fusion.96 = f32[4,4,64,4096]{3,2,1,0:T(8,128)} fusion(f32[4,4,64,4096]{3,2,1,0:T(8,128)} %get-tuple-element.266, s32[]{:T(128)S(6)} %copy.48, bf16[4,768,4096]{2,1,0:T(8,128)(2,1)} %reshape.71, bf16[2,768,64]{1,2,0:T(8,128)(2,1)S(1)} %get-tuple-element.288, s32[]{:T(128)S(6)} %select_n.409), kind=kOutput, calls=%fused_computation.29.clone.1 | convolution fusion | flops 1610612736 | bytes 29458440 | tf_op jit(solution)/shard_map/while/body/eval_jaxpr/io,fir->for/dot_general | solution.py:86
  263.3 11.5 %fusion.93 = (bf16[4,2,1,32,16,256]{5,4,3,2,1,0:T(8,128)(2,1)S(1)}, bf16[4,2,1,32,16,256]{5,4,3,2,1,0:T(8,128)(2,1)S(1)}, bf16[4,2,1,32,16,256]{5,4,3,2,1,0:T(8,128)(2,1)S(1)}, bf16[4,2,1,32,16,256]{5,4,3,2,1,0:T(8,128)(2,1)S(1)}) fusion(s32[]{:T(128)S(6)} %select_n.402, bf16[4,2,32,16,256]{4,3,2,1,0:T(8,128)(2,1)} %get-tuple-element.233, ...), kind=kLoop, calls=%fused_computation.34.clone.1 | loop fusion | flops 16777216 | bytes 10485776 | tf_op jit(solution)/shard_map/while/body/eval_jaxpr/stack | solution.py:76
  298.5 10.3 pad_maximum_fusion.3
  308.8 37.8 %reshape.71 = bf16[4,768,4096]{2,1,0:T(8,128)(2,1)} reshape(bf16[4,2,3,4,32,16,256]{6,5,4,3,2,1,0:T(8,128)(2,1)} %pad_maximum_fusion.3) | data formatting | bytes 50331648 | tf_op jit(solution)/shard_map/while/body/eval_jaxpr/reshape | solution.py:84
  349.1 14.7 %fusion.96 = f32[4,4,64,4096]{3,2,1,0:T(8,128)} fusion(f32[4,4,64,4096]{3,2,1,0:T(8,128)} %get-tuple-element.266, s32[]{:T(128)S(6)} %copy.48, bf16[4,768,4096]{2,1,0:T(8,128)(2,1)} %reshape.71, bf16[2,768,64]{1,2,0:T(8,128)(2,1)S(1)} %get-tuple-element.288, s32[]{:T(128)S(6)} %select_n.409), kind=kOutput, calls=%fused_computation.29.clone.1 | convolution fusion | flops 1610612736 | bytes 29458440 | tf_op jit(solution)/shard_map/while/body/eval_jaxpr/io,fir->for/dot_general | solution.py:86
  369.4 11.5 %fusion.93 = (bf16[4,2,1,32,16,256]{5,4,3,2,1,0:T(8,128)(2,1)S(1)}, bf16[4,2,1,32,16,256]{5,4,3,2,1,0:T(8,128)(2,1)S(1)}, bf16[4,2,1,32,16,256]{5,4,3,2,1,0:T(8,128)(2,1)S(1)}, bf16[4,2,1,32,16,256]{5,4,3,2,1,0:T(8,128)(2,1)S(1)}) fusion(s32[]{:T(128)S(6)} %select_n.402, bf16[4,2,32,16,256]{4,3,2,1,0:T(8,128)(2,1)} %get-tuple-element.233, ...), kind=kLoop, calls=%fused_computation.34.clone.1 | loop fusion | flops 16777216 | bytes 10485776 | tf_op jit(solution)/shard_map/while/body/eval_jaxpr/stack | solution.py:76
  404.5 10.3 pad_maximum_fusion.3
  414.9 37.8 %reshape.71 = bf16[4,768,4096]{2,1,0:T(8,128)(2,1)} reshape(bf16[4,2,3,4,32,16,256]{6,5,4,3,2,1,0:T(8,128)(2,1)} %pad_maximum_fusion.3) | data formatting | bytes 50331648 | tf_op jit(solution)/shard_map/while/body/eval_jaxpr/reshape | solution.py:84
  455.2 14.7 %fusion.96 = f32[4,4,64,4096]{3,2,1,0:T(8,128)} fusion(f32[4,4,64,4096]{3,2,1,0:T(8,128)} %get-tuple-element.266, s32[]{:T(128)S(6)} %copy.48, bf16[4,768,4096]{2,1,0:T(8,128)(2,1)} %reshape.71, bf16[2,768,64]{1,2,0:T(8,128)(2,1)S(1)} %get-tuple-element.288, s32[]{:T(128)S(6)} %select_n.409), kind=kOutput, calls=%fused_computation.29.clone.1 | convolution fusion | flops 1610612736 | bytes 29458440 | tf_op jit(solution)/shard_map/while/body/eval_jaxpr/io,fir->for/dot_general | solution.py:86
  470.3 11.0 %copy.40 = f32[128,8,16,256]{3,2,1,0:T(8,128)S(1)} copy(f32[128,8,16,256]{3,1,2,0:T(8,128)} %bitcast.156) | data formatting | bytes 33554432
  487.5 17.8 %fusion.30 = f32[5,2,32,16,256]{4,0,3,2,1:T(8,128)} fusion(f32[16,2,32,16,256]{4,3,2,1,0:T(8,128)S(1)} %convert_select_fusion, f32[5,16]{1,0:T(8,128)S(1)} %copy-done), kind=kOutput, calls=%fused_computation.64 | convolution fusion | flops 251658240 | bytes 22020416 | tf_op jit(solution)/shard_map/bf,fpcrx->bpcrx/dot_general | solution.py:92
  505.3 15.1 %copy.30 = f32[5,2,32,16,256]{2,4,3,1,0:T(8,128)} copy(f32[5,2,32,16,256]{4,0,3,2,1:T(8,128)} %fusion.30) | data formatting | bytes 10485760 | tf_op jit(solution)/shard_map/bf,fpcrx->bpcrx/dot_general | solution.py:92
  520.4 13.4 %dynamic-slice_bitcast_fusion.1 = (f32[1,5,2,32,16,16]{3,5,0,4,2,1:T(8,128)S(1)}, f32[1,5,2,32,16,16]{3,5,0,4,2,1:T(8,128)S(1)}, f32[1,5,2,32,16,16]{3,5,0,4,2,1...) fusion(f32[5,2,32,16,16,16]{2,5,4,3,1,0:T(8,128)} %bitcast.150,, ...), kind=kLoop, calls=%fused_computation.75 | loop fusion | bytes 9830460 | tf_op jit(solution)/shard_map/jit(dynamic_index_in_dim)/dynamic_slice | solution.py:100
  539.4 24.3 %collective-permute-done.2 = f32[1,5,2,32,16,16]{3,5,0,4,2,1:T(8,128)} collective-permute-done((f32[1,5,2,32,16,16]{3,5,0,4,2,1:T(8,128)}, f32[1,5,2,32,16,16]{3,5,0,4,2,1:T(8,128)}, u32[]{:S(2)}, u32[]{:S(2)}) %collective-permute-start.2) | collective-permute-done | bytes 327712 | tf_op jit(solution)/shard_map/ppermute | solution.py:101
  566.2 25.9 %collective-permute-done.3 = f32[1,5,2,32,16,16]{3,5,0,4,2,1:T(8,128)} collective-permute-done((f32[1,5,2,32,16,16]{3,5,0,4,2,1:T(8,128)}, f32[1,5,2,32,16,16]{3,5,0,4,2,1:T(8,128)}, u32[]{:S(2)}, u32[]{:S(2)}) %collective-permute-start.3) | collective-permute-done | bytes 327712 | tf_op jit(solution)/shard_map/ppermute | solution.py:101
  599.4 26.1 %collective-permute-start.10 = (f32[1,5,2,32,16,16]{3,5,0,4,2,1:T(8,128)S(1)}, f32[1,5,2,32,16,16]{3,5,0,4,2,1:T(8,128)S(1)}, u32[]{:S(2)}, u32[]{:S(2)}) collective-permute-start(f32[1,5,2,32,16,16]{3,5,0,4,2,1:T(8,128)S(1)} %copy-done.7), channel_id=1, source_target_pairs={{0,9},{1,10},{2,11},{3,12},{4,13},{5,14},{6,15},{7,0},{8,1},{9,2},... | collective-permute-start | bytes 983048 | tf_op jit(solution)/shard_map/ppermute | solution.py:101
  626.7 34.3 %collective-permute-start.11 = (f32[1,5,2,32,16,16]{3,5,0,4,2,1:T(8,128)S(1)}, f32[1,5,2,32,16,16]{3,5,0,4,2,1:T(8,128)S(1)}, u32[]{:S(2)}, u32[]{:S(2)}) collective-permute-start(f32[1,5,2,32,16,16]{3,5,0,4,2,1:T(8,128)S(1)} %copy-done.6), channel_id=1, source_target_pairs={{0,10},{1,11},{2,12},{3,13},{4,14},{5,15},{6,0},{7,1},{8,2},{9,3},... | collective-permute-start | bytes 983048 | tf_op jit(solution)/shard_map/ppermute | solution.py:101
  662.2 27.2 %collective-permute-done.7 = f32[1,5,2,32,16,16]{3,5,0,4,2,1:T(8,128)S(1)} collective-permute-done((f32[1,5,2,32,16,16]{3,5,0,4,2,1:T(8,128)}, f32[1,5,2,32,16,16]{3,5,0,4,2,1:T(8,128)S(1)}, u32[]{:S(2)}, u32[]{:S(2)}) %collective-permute-start.7) | collective-permute-done | bytes 327712 | tf_op jit(solution)/shard_map/ppermute | solution.py:101
  689.5 95.7 %collective-permute-start.12 = (f32[1,5,2,32,16,16]{3,5,0,4,2,1:T(8,128)S(1)}, f32[1,5,2,32,16,16]{3,5,0,4,2,1:T(8,128)S(1)}, u32[]{:S(2)}, u32[]{:S(2)}) collective-permute-start(f32[1,5,2,32,16,16]{3,5,0,4,2,1:T(8,128)S(1)} %copy-done.5), channel_id=1, source_target_pairs={{0,11},{1,12},{2,13},{3,14},{4,15},{5,0},{6,1},{7,2},{8,3},{9,4},{... | collective-permute-start | bytes 983048 | tf_op jit(solution)/shard_map/ppermute | solution.py:101
  786.4 80.1 %collective-permute-start.13 = (f32[1,5,2,32,16,16]{3,5,0,4,2,1:T(8,128)S(1)}, f32[1,5,2,32,16,16]{3,5,0,4,2,1:T(8,128)S(1)}, u32[]{:S(2)}, u32[]{:S(2)}) collective-permute-start(f32[1,5,2,32,16,16]{3,5,0,4,2,1:T(8,128)S(1)} %copy-done.4), channel_id=1, source_target_pairs={{0,12},{1,13},{2,14},{3,15},{4,0},{5,1},{6,2},{7,3},{8,4},{9,5},{1... | collective-permute-start | bytes 983048 | tf_op jit(solution)/shard_map/ppermute | solution.py:101
  867.7 62.7 %collective-permute-start.14 = (f32[1,5,2,32,16,16]{3,5,0,4,2,1:T(8,128)S(1)}, f32[1,5,2,32,16,16]{3,5,0,4,2,1:T(8,128)S(1)}, u32[]{:S(2)}, u32[]{:S(2)}) collective-permute-start(f32[1,5,2,32,16,16]{3,5,0,4,2,1:T(8,128)S(1)} %copy-done.3), channel_id=1, source_target_pairs={{0,13},{1,14},{2,15},{3,0},{4,1},{5,2},{6,3},{7,4},{8,5},{9,6},{10... | collective-permute-start | bytes 983048 | tf_op jit(solution)/shard_map/ppermute | solution.py:101
  933.0 41.0 %collective-permute-start.16 = (f32[1,5,2,32,16,16]{3,5,0,4,2,1:T(8,128)S(1)}, f32[1,5,2,32,16,16]{3,5,0,4,2,1:T(8,128)S(1)}, u32[]{:S(2)}, u32[]{:S(2)}) collective-permute-start(f32[1,5,2,32,16,16]{3,5,0,4,2,1:T(8,128)S(1)} %get-tuple-element.140), channel_id=1, source_target_pairs={{0,15},{1,0},{2,1},{3,2},{4,3},{5,4},{6,5},{7,6},{8,7},{9,8},{10,9... | collective-permute-start | bytes 983048 | tf_op jit(solution)/shard_map/ppermute | solution.py:101
  979.0 41.1 %collective-permute-done.15 = f32[1,5,2,32,16,16]{3,5,0,4,2,1:T(8,128)S(1)} collective-permute-done((f32[1,5,2,32,16,16]{3,5,0,4,2,1:T(8,128)S(1)}, f32[1,5,2,32,16,16]{3,5,0,4,2,1:T(8,128)S(1)}, u32[]{:S(2)}, u32[]{:S(2)}) %collective-permute-start.15) | collective-permute-done | bytes 327712 | tf_op jit(solution)/shard_map/ppermute | solution.py:101
  (121 shorter events, 241.5 us)
Async XLA Ops:
  0.0 487.5 %copy-start = (f32[5,16]{1,0:T(8,128)S(1)}, f32[5,16]{1,0:T(8,128)}, u32[]{:S(2)}) copy-start(f32[5,16]{1,0:T(8,128)} %param.15) | copy-start | bytes 964
  1.5 7.3 copy-start.10
  8.8 10.7 copy-start.12
  13.5 16.2 %collective-permute-start.1 = (bf16[16,2,32,1,256]{4,2,3,1,0:T(8,128)(2,1)S(1)}, bf16[16,2,32,1,256]{4,2,3,1,0:T(8,128)(2,1)S(1)}, u32[]{:S(2)}, u32[]{:S(2)}) collective-permute-start(bf16[16,2,32,1,256]{4,2,3,1,0:T(8,128)(2,1)S(1)} %copy.26), channel_id=1, source_target_pairs={{1,0},{2,1},{3,2},{4,3},{5,4},{6,5},{7,6},{8,7},{9,8},{10,9},{11,1... | collective-permute-start | bytes 1572872 | tf_op jit(solution)/shard_map/ppermute | solution.py:32
  16.2 14.5 %collective-permute-start = (bf16[16,2,32,1,256]{4,2,3,1,0:T(8,128)(2,1)S(1)}, bf16[16,2,32,1,256]{4,2,3,1,0:T(8,128)(2,1)S(1)}, u32[]{:S(2)}, u32[]{:S(2)}) collective-permute-start(bf16[16,2,32,1,256]{4,2,3,1,0:T(8,128)(2,1)S(1)} %copy.25), channel_id=1, source_target_pairs={{0,1},{1,2},{2,3},{3,4},{4,5},{5,6},{6,7},{7,8},{8,9},{9,10},{10,1... | collective-permute-start | bytes 1572872 | tf_op jit(solution)/shard_map/ppermute | solution.py:29
  31.8 13.5 %copy-start.9 = (bf16[2,768,64]{1,2,0:T(8,128)(2,1)S(1)}, bf16[2,768,64]{1,2,0:T(8,128)(2,1)}, u32[]{:S(2)}) copy-start(bf16[2,768,64]{1,2,0:T(8,128)(2,1)} %param.11) | copy-start | bytes 589828
  168.8 1.6 copy-start.1
  274.9 1.6 copy-start.1
  380.9 1.6 copy-start.1
  470.3 11.0 %copy-start.11 = (pred[16,16]{1,0:T(8,128)(4,1)S(1)}, pred[16,16]{1,0:T(8,128)(4,1)}, u32[]{:S(2)}) copy-start(pred[16,16]{1,0:T(8,128)(4,1)} %copy-done.10) | copy-start | bytes 772
  533.8 29.9 %collective-permute-start.2 = (f32[1,5,2,32,16,16]{3,5,0,4,2,1:T(8,128)}, f32[1,5,2,32,16,16]{3,5,0,4,2,1:T(8,128)}, u32[]{:S(2)}, u32[]{:S(2)}) collective-permute-start(f32[1,5,2,32,16,16]{3,5,0,4,2,1:T(8,128)} %get-tuple-element.154), channel_id=1, source_target_pairs={{0,1},{1,2},{2,3},{3,4},{4,5},{5,6},{6,7},{7,8},{8,9},{9,10},{10,1... | collective-permute-start | bytes 983048 | tf_op jit(solution)/shard_map/ppermute | solution.py:101
  535.4 56.7 %collective-permute-start.3 = (f32[1,5,2,32,16,16]{3,5,0,4,2,1:T(8,128)}, f32[1,5,2,32,16,16]{3,5,0,4,2,1:T(8,128)}, u32[]{:S(2)}, u32[]{:S(2)}) collective-permute-start(f32[1,5,2,32,16,16]{3,5,0,4,2,1:T(8,128)} %get-tuple-element.153), channel_id=1, source_target_pairs={{0,2},{1,3},{2,4},{3,5},{4,6},{5,7},{6,8},{7,9},{8,10},{9,11},{10,... | collective-permute-start | bytes 983048 | tf_op jit(solution)/shard_map/ppermute | solution.py:101
  535.4 59.2 %collective-permute-start.4 = (f32[1,5,2,32,16,16]{3,5,0,4,2,1:T(8,128)}, f32[1,5,2,32,16,16]{3,5,0,4,2,1:T(8,128)}, u32[]{:S(2)}, u32[]{:S(2)}) collective-permute-start(f32[1,5,2,32,16,16]{3,5,0,4,2,1:T(8,128)} %get-tuple-element.152), channel_id=1, source_target_pairs={{0,3},{1,4},{2,5},{3,6},{4,7},{5,8},{6,9},{7,10},{8,11},{9,12},{10... | collective-permute-start | bytes 983048 | tf_op jit(solution)/shard_map/ppermute | solution.py:101
  537.0 57.6 %copy-start.8 = (f32[1,5,2,32,16,16]{3,5,0,4,2,1:T(8,128)S(1)}, f32[1,5,2,32,16,16]{3,5,0,4,2,1:T(8,128)}, u32[]{:S(2)}) copy-start(f32[1,5,2,32,16,16]{3,5,0,4,2,1:T(8,128)} %get-tuple-element.147) | copy-start | bytes 983044
  537.0 62.3 %copy-start.7 = (f32[1,5,2,32,16,16]{3,5,0,4,2,1:T(8,128)S(1)}, f32[1,5,2,32,16,16]{3,5,0,4,2,1:T(8,128)}, u32[]{:S(2)}) copy-start(f32[1,5,2,32,16,16]{3,5,0,4,2,1:T(8,128)} %get-tuple-element.146) | copy-start | bytes 983044
  537.0 62.3 %collective-permute-start.5 = (f32[1,5,2,32,16,16]{3,5,0,4,2,1:T(8,128)}, f32[1,5,2,32,16,16]{3,5,0,4,2,1:T(8,128)S(1)}, u32[]{:S(2)}, u32[]{:S(2)}) collective-permute-start(f32[1,5,2,32,16,16]{3,5,0,4,2,1:T(8,128)} %get-tuple-element.151), channel_id=1, source_target_pairs={{0,4},{1,5},{2,6},{3,7},{4,8},{5,9},{6,10},{7,11},{8,12},{9,13},{1... | collective-permute-start | bytes 983048 | tf_op jit(solution)/shard_map/ppermute | solution.py:101
  537.1 89.6 %collective-permute-start.6 = (f32[1,5,2,32,16,16]{3,5,0,4,2,1:T(8,128)}, f32[1,5,2,32,16,16]{3,5,0,4,2,1:T(8,128)S(1)}, u32[]{:S(2)}, u32[]{:S(2)}) collective-permute-start(f32[1,5,2,32,16,16]{3,5,0,4,2,1:T(8,128)} %get-tuple-element.150), channel_id=1, source_target_pairs={{0,5},{1,6},{2,7},{3,8},{4,9},{5,10},{6,11},{7,12},{8,13},{9,14},{... | collective-permute-start | bytes 983048 | tf_op jit(solution)/shard_map/ppermute | solution.py:101
  563.7 125.8 %collective-permute-start.7 = (f32[1,5,2,32,16,16]{3,5,0,4,2,1:T(8,128)}, f32[1,5,2,32,16,16]{3,5,0,4,2,1:T(8,128)S(1)}, u32[]{:S(2)}, u32[]{:S(2)}) collective-permute-start(f32[1,5,2,32,16,16]{3,5,0,4,2,1:T(8,128)} %get-tuple-element.149), channel_id=1, source_target_pairs={{0,6},{1,7},{2,8},{3,9},{4,10},{5,11},{6,12},{7,13},{8,14},{9,15},... | collective-permute-start | bytes 983048 | tf_op jit(solution)/shard_map/ppermute | solution.py:101
  566.2 60.5 %copy-start.6 = (f32[1,5,2,32,16,16]{3,5,0,4,2,1:T(8,128)S(1)}, f32[1,5,2,32,16,16]{3,5,0,4,2,1:T(8,128)}, u32[]{:S(2)}) copy-start(f32[1,5,2,32,16,16]{3,5,0,4,2,1:T(8,128)} %get-tuple-element.145) | copy-start | bytes 983044
  592.1 194.4 %collective-permute-start.8 = (f32[1,5,2,32,16,16]{3,5,0,4,2,1:T(8,128)}, f32[1,5,2,32,16,16]{3,5,0,4,2,1:T(8,128)S(1)}, u32[]{:S(2)}, u32[]{:S(2)}) collective-permute-start(f32[1,5,2,32,16,16]{3,5,0,4,2,1:T(8,128)} %get-tuple-element.148), channel_id=1, source_target_pairs={{0,7},{1,8},{2,9},{3,10},{4,11},{5,12},{6,13},{7,14},{8,15},{9,0},... | collective-permute-start | bytes 983048 | tf_op jit(solution)/shard_map/ppermute | solution.py:101
  594.6 94.9 %copy-start.5 = (f32[1,5,2,32,16,16]{3,5,0,4,2,1:T(8,128)S(1)}, f32[1,5,2,32,16,16]{3,5,0,4,2,1:T(8,128)}, u32[]{:S(2)}) copy-start(f32[1,5,2,32,16,16]{3,5,0,4,2,1:T(8,128)} %get-tuple-element.144) | copy-start | bytes 983044
  594.6 273.1 %collective-permute-start.9 = (f32[1,5,2,32,16,16]{3,5,0,4,2,1:T(8,128)S(1)}, f32[1,5,2,32,16,16]{3,5,0,4,2,1:T(8,128)S(1)}, u32[]{:S(2)}, u32[]{:S(2)}) collective-permute-start(f32[1,5,2,32,16,16]{3,5,0,4,2,1:T(8,128)S(1)} %copy-done.8), channel_id=1, source_target_pairs={{0,8},{1,9},{2,10},{3,11},{4,12},{5,13},{6,14},{7,15},{8,0},{9,1},... | collective-permute-start | bytes 983048 | tf_op jit(solution)/shard_map/ppermute | solution.py:101
  599.4 187.0 %copy-start.4 = (f32[1,5,2,32,16,16]{3,5,0,4,2,1:T(8,128)S(1)}, f32[1,5,2,32,16,16]{3,5,0,4,2,1:T(8,128)}, u32[]{:S(2)}) copy-start(f32[1,5,2,32,16,16]{3,5,0,4,2,1:T(8,128)} %get-tuple-element.143) | copy-start | bytes 983044
  599.4 332.4 %collective-permute-start.10 = (f32[1,5,2,32,16,16]{3,5,0,4,2,1:T(8,128)S(1)}, f32[1,5,2,32,16,16]{3,5,0,4,2,1:T(8,128)S(1)}, u32[]{:S(2)}, u32[]{:S(2)}) collective-permute-start(f32[1,5,2,32,16,16]{3,5,0,4,2,1:T(8,128)S(1)} %copy-done.7), channel_id=1, source_target_pairs={{0,9},{1,10},{2,11},{3,12},{4,13},{5,14},{6,15},{7,0},{8,1},{9,2},... | collective-permute-start | bytes 983048 | tf_op jit(solution)/shard_map/ppermute | solution.py:101
  626.7 241.1 %copy-start.3 = (f32[1,5,2,32,16,16]{3,5,0,4,2,1:T(8,128)S(1)}, f32[1,5,2,32,16,16]{3,5,0,4,2,1:T(8,128)}, u32[]{:S(2)}) copy-start(f32[1,5,2,32,16,16]{3,5,0,4,2,1:T(8,128)} %get-tuple-element.142) | copy-start | bytes 983044
  626.7 306.3 %collective-permute-start.11 = (f32[1,5,2,32,16,16]{3,5,0,4,2,1:T(8,128)S(1)}, f32[1,5,2,32,16,16]{3,5,0,4,2,1:T(8,128)S(1)}, u32[]{:S(2)}, u32[]{:S(2)}) collective-permute-start(f32[1,5,2,32,16,16]{3,5,0,4,2,1:T(8,128)S(1)} %copy-done.6), channel_id=1, source_target_pairs={{0,10},{1,11},{2,12},{3,13},{4,14},{5,15},{6,0},{7,1},{8,2},{9,3},... | collective-permute-start | bytes 983048 | tf_op jit(solution)/shard_map/ppermute | solution.py:101
  689.5 285.8 %collective-permute-start.12 = (f32[1,5,2,32,16,16]{3,5,0,4,2,1:T(8,128)S(1)}, f32[1,5,2,32,16,16]{3,5,0,4,2,1:T(8,128)S(1)}, u32[]{:S(2)}, u32[]{:S(2)}) collective-permute-start(f32[1,5,2,32,16,16]{3,5,0,4,2,1:T(8,128)S(1)} %copy-done.5), channel_id=1, source_target_pairs={{0,11},{1,12},{2,13},{3,14},{4,15},{5,0},{6,1},{7,2},{8,3},{9,4},{... | collective-permute-start | bytes 983048 | tf_op jit(solution)/shard_map/ppermute | solution.py:101
  786.4 190.1 %collective-permute-start.13 = (f32[1,5,2,32,16,16]{3,5,0,4,2,1:T(8,128)S(1)}, f32[1,5,2,32,16,16]{3,5,0,4,2,1:T(8,128)S(1)}, u32[]{:S(2)}, u32[]{:S(2)}) collective-permute-start(f32[1,5,2,32,16,16]{3,5,0,4,2,1:T(8,128)S(1)} %copy-done.4), channel_id=1, source_target_pairs={{0,12},{1,13},{2,14},{3,15},{4,0},{5,1},{6,2},{7,3},{8,4},{9,5},{1... | collective-permute-start | bytes 983048 | tf_op jit(solution)/shard_map/ppermute | solution.py:101
  867.7 110.0 %collective-permute-start.14 = (f32[1,5,2,32,16,16]{3,5,0,4,2,1:T(8,128)S(1)}, f32[1,5,2,32,16,16]{3,5,0,4,2,1:T(8,128)S(1)}, u32[]{:S(2)}, u32[]{:S(2)}) collective-permute-start(f32[1,5,2,32,16,16]{3,5,0,4,2,1:T(8,128)S(1)} %copy-done.3), channel_id=1, source_target_pairs={{0,13},{1,14},{2,15},{3,0},{4,1},{5,2},{6,3},{7,4},{8,5},{9,6},{10... | collective-permute-start | bytes 983048 | tf_op jit(solution)/shard_map/ppermute | solution.py:101
  931.8 88.4 %collective-permute-start.15 = (f32[1,5,2,32,16,16]{3,5,0,4,2,1:T(8,128)S(1)}, f32[1,5,2,32,16,16]{3,5,0,4,2,1:T(8,128)S(1)}, u32[]{:S(2)}, u32[]{:S(2)}) collective-permute-start(f32[1,5,2,32,16,16]{3,5,0,4,2,1:T(8,128)S(1)} %get-tuple-element.141), channel_id=1, source_target_pairs={{0,14},{1,15},{2,0},{3,1},{4,2},{5,3},{6,4},{7,5},{8,6},{9,7},{10,... | collective-permute-start | bytes 983048 | tf_op jit(solution)/shard_map/ppermute | solution.py:101
  933.0 91.0 %collective-permute-start.16 = (f32[1,5,2,32,16,16]{3,5,0,4,2,1:T(8,128)S(1)}, f32[1,5,2,32,16,16]{3,5,0,4,2,1:T(8,128)S(1)}, u32[]{:S(2)}, u32[]{:S(2)}) collective-permute-start(f32[1,5,2,32,16,16]{3,5,0,4,2,1:T(8,128)S(1)} %get-tuple-element.140), channel_id=1, source_target_pairs={{0,15},{1,0},{2,1},{3,2},{4,3},{5,4},{6,5},{7,6},{8,7},{9,8},{10,9... | collective-permute-start | bytes 983048 | tf_op jit(solution)/shard_map/ppermute | solution.py:101
  1067.7 5.1 copy-start.2
  (1 other events, 1.6 us)
